TPU v7x, 16 devices: a whole 2x2x2 slice. The times are simulated.
16 devices in a mesh: data: 16 (over z, y, x, core).
Axes of the slice: x: 2, y: 2, z: 2, core: 2. Of those that a mesh axis runs over, the one named last changes fastest.
Arguments:
- x_in: bfloat16 [65536, 1024], P('data')
- d_out: bfloat16 [65536, 1024], P('data')
- w_stack: bfloat16 [4, 1024, 1024], replicated
- a_old: float32 [4, 1024, 1024], replicated
- s_old: float32 [4, 1024, 1024], replicated
- a_inv: float32 [4, 1024, 1024], replicated
- s_inv: float32 [4, 1024, 1024], replicated
Outputs:
- output 1: float32 [4, 1024, 1024], replicated
- output 2: float32 [4, 1024, 1024], replicated
- output 3: float32 [4, 1024, 1024], replicated
All inputs are finite; a program needn't handle non-finite values.
Results may differ from a plain program's by a relative error of at most 0.00138593.
Values are sent between devices in bfloat16 or wider.
A program may use at most 1 GiB of HBM per device.

v0:
```python
import functools

import jax
import jax.numpy as jnp
from jax import lax
from jax.experimental import pallas as pl
from jax.experimental.pallas import tpu as pltpu
from jax.sharding import PartitionSpec as P

RHO = 0.75
ERF_SCALE = 0.7071067811865476
PDF_SCALE = 0.3989422804014327
D = 1024
B = 256
NT = 8
F32 = jnp.float32
BF16 = jnp.bfloat16

SYM_BLOCKS = [(bi, bj) for bj in range(4) for bi in range(bj + 1)]
NB = len(SYM_BLOCKS) - 1
Q = B // 2
DIAG = [SYM_BLOCKS.index((i, i)) for i in range(4)]
CARRIED = [(0, 0), (0, 1), (1, 1)]


def dot_f32(lhs, rhs, dims=((1,), (0,)), precision=None):
    return lax.dot_general(lhs, rhs, (dims, ((), ())), precision=precision, preferred_element_type=F32)


class Unit:
    def __init__(self, kind, layer, slot, first, gaps, rot):
        self.kind, self.old, self.layer, self.slot = ("full" if kind == "w" else "sym"), kind, layer, slot
        self.out = layer + (4 if kind == "s" else 0)
        self.hooks = [first]
        for gap in gaps:
            self.hooks.append(self.hooks[-1] + int(gap))
        if self.kind == "sym":
            sizes = [3, 3, 3]
        else:
            sizes = [384, 384, 384]
            sizes[rot % 3] = 256
        starts = [0, sizes[0], sizes[0] + sizes[1]]
        self.groups = list(zip(starts, sizes))


U_PIECES = 8
U_START = 22

UNITS = [
    Unit("s", 3, 0, 9, "35421232", 0),
    Unit("a", 1, 2, 26, "74222784", 0),
    Unit("a", 3, 1, 42, "46315283", 0),
    Unit("w", 3, 0, 48, "03311151", 0),
    Unit("s", 1, 0, 67, "08993561", 0),
    Unit("a", 0, 1, 16, "14222462", 0),
    Unit("a", 2, 0, 34, "13223984", 0),
    Unit("s", 0, 1, 79, "53542257", 0),
    Unit("w", 0, 1, 76, "16174220", 0),
    Unit("w", 1, 0, 64, "12782571", 2),
    Unit("w", 2, 1, 56, "03311143", 1),
    Unit("s", 2, 2, 68, "08579225", 0),
]


def step_kernel(tm, tokens, x_hbm, dy_hbm, w_hbm, aold_hbm, sold_hbm, ainv_hbm, sinv_hbm,
                osym, ovt, u_hbm, z_hbm, h_hbm,
                cur, ht, w_buf, st_a, st_b, ainv_buf, sinv_buf, vt_buf, u_buf,
                sacc, facc, sr0, sr1, sr2, sr3, fr0, fr1, fr2, fr3, old_buf, spc, fpc,
                send_sem, recv_sem, loc_sem, old_sem, x_sem, h_sem, w_sem, sta_sem, stb_sem, z_sem, ainv_sem, sinv_sem, vt_sem, u_sem, u_send_sem, u_recv_sem):
    z_out = st_b
    me = lax.axis_index("data")
    core = lax.rem(me, 2)
    pos = [lax.rem(me // 2, 2), lax.rem(me // 4, 2), lax.rem(me // 8, 2)]
    core_peer = me + 1 - 2 * core
    peers = [me + (1 - 2 * pos[d]) * (2 << d) for d in range(3)]

    sym_recv = [sr0, sr1, sr2, sr3]
    full_recv = [fr0, fr1, fr2, fr3]

    def dims_of(g):
        return [g, (g + 1) % 3, (g + 2) % 3]

    def base_size(u, g):
        return (0, B) if u.kind == "sym" else u.groups[g]

    def offset(u, g, level):
        r0, n = base_size(u, g)
        bits = [core] + [pos[d] for d in dims_of(g)]
        off = r0
        for i in range(level):
            off = off + bits[i] * (n >> (i + 1))
        return pl.multiple_of(off, 8) if level else off

    def other(u, g, level):
        r0, n = base_size(u, g)
        bits = [core] + [pos[d] for d in dims_of(g)]
        return pl.multiple_of(offset(u, g, level) + (1 - bits[level]) * (n >> (level + 1)), 8)

    def peer(g, level):
        return core_peer if level == 0 else peers[dims_of(g)[level - 1]]

    def rows(u, g, level):
        return base_size(u, g)[1] >> level

    def acc_at(u, g, off, size):
        if u.kind == "sym":
            b0, nb = u.groups[g]
            return sacc.at[u.slot, pl.ds(b0, nb), pl.ds(off, size), :]
        return facc.at[u.slot, pl.ds(off, size), :]

    def recv_at(u, g, level, start=0, size=None):
        size = size or rows(u, g, level + 1)
        if u.kind == "sym":
            b0, nb = u.groups[g]
            return sym_recv[level].at[u.slot, pl.ds(b0, nb), pl.ds(start, size), :]
        return full_recv[level].at[u.slot, pl.ds((u.groups[g][0] >> (level + 1)) + start, size), :]

    def add_received(u, g, level):
        size = rows(u, g, level + 1)
        chunk = next(c for c in (32, 16, 8) if size % c == 0)
        mine = offset(u, g, level + 1)

        def body(i, carry):
            start = pl.multiple_of(i * chunk, 8)
            ref = acc_at(u, g, pl.multiple_of(mine + start, 8), chunk)
            ref[...] = ref[...] + recv_at(u, g, level, start, chunk)[...]
            return carry

        lax.fori_loop(0, size // chunk, body, 0)

    def piece_at(u, g):
        if u.kind == "sym":
            b0, nb = u.groups[g]
            return spc.at[u.slot, pl.ds(b0, nb)]
        r0, n = u.groups[g]
        return fpc.at[u.slot, pl.ds(r0 >> 4, n >> 4), :]

    def out_at(u, g, off, size):
        if u.kind == "sym":
            b0, nb = u.groups[g]
            return osym.at[u.out, pl.ds(b0, nb), pl.ds(off, size), :]
        return ovt.at[u.out, pl.ds(off, size), :]

    def sem_row(u):
        return u.slot if u.kind == "sym" else 3 + u.slot

    def rs_copy(u, g, level):
        return pltpu.make_async_remote_copy(
            src_ref=acc_at(u, g, other(u, g, level), rows(u, g, level + 1)), dst_ref=recv_at(u, g, level),
            send_sem=send_sem.at[sem_row(u), g], recv_sem=recv_sem.at[sem_row(u), level, g],
            device_id=(peer(g, level),), device_id_type=pl.DeviceIdType.MESH)

    def ag_copy(u, g, level):
        off, size = offset(u, g, level + 1), rows(u, g, level + 1)
        src = piece_at(u, g) if level == 3 else out_at(u, g, off, size)
        return pltpu.make_async_remote_copy(
            src_ref=src, dst_ref=out_at(u, g, off, size),
            send_sem=send_sem.at[sem_row(u), g], recv_sem=recv_sem.at[sem_row(u), 7 - level, g],
            device_id=(peer(g, level),), device_id_type=pl.DeviceIdType.MESH)

    def own_copy(u, g):
        return pltpu.make_async_copy(piece_at(u, g), out_at(u, g, offset(u, g, 4), rows(u, g, 4)), loc_sem.at[sem_row(u), g])

    def old_copies(u):
        src = aold_hbm if u.old == "a" else sold_hbm
        for g in range(3):
            b0, nb = u.groups[g]
            for b in range(b0, b0 + nb):
                bi, bj = SYM_BLOCKS[b]
                row = pl.multiple_of(bi * B + offset(u, g, 4), 8)
                for half in range(2):
                    from_row, from_col = row, bj * B + half * Q
                    if bi == bj and half == 0:
                        c_row, c_col = CARRIED[bi]
                        from_row = pl.multiple_of(row + core * ((3 - bi) * B - Q + c_row * Q), 8)
                        from_col = pl.multiple_of(from_col + core * ((3 - bi) * B + c_col * Q), Q)
                    pltpu.make_async_copy(src.at[u.layer, pl.ds(from_row, 16), pl.ds(from_col, Q)], old_buf.at[u.slot, b, :, pl.ds(half * Q, Q)], old_sem.at[u.slot]).start()

    def ainv_copy(layer):
        return pltpu.make_async_copy(ainv_hbm.at[layer], ainv_buf, ainv_sem)

    def event(u, e):
        if e == 0:
            if u.kind == "sym":
                for i, (c_row, c_col) in enumerate(CARRIED):
                    sacc[u.slot, DIAG[i], Q:, :Q] = sacc[u.slot, NB, c_row * Q:(c_row + 1) * Q, c_col * Q:(c_col + 1) * Q]
            for g in range(3):
                rs_copy(u, g, 0).start()
            if u.kind == "sym":
                old_copies(u)
            return
        if e <= 4:
            level = e - 1
            for g in range(3):
                rs_copy(u, g, level).wait_recv()
                rs_copy(u, g, level).wait_send()
                if e < 4:
                    add_received(u, g, level)
                    rs_copy(u, g, level + 1).start()
            if e == 4:
                if u.kind == "sym":
                    pltpu.make_async_copy(osym.at[u.out, :, pl.ds(0, 16), :], old_buf.at[u.slot], old_sem.at[u.slot]).wait()
                for g in range(3):
                    total = acc_at(u, g, offset(u, g, 4), rows(u, g, 4))[...] + recv_at(u, g, 3)[...]
                    if u.kind == "sym":
                        b0, nb = u.groups[g]
                        piece_at(u, g)[...] = RHO * old_buf[u.slot, pl.ds(b0, nb)] + (1.0 - RHO) * (total / tokens)
                    else:
                        piece_at(u, g)[...] = total / tokens
                if u.kind == "full":
                    ainv_copy(u.layer).wait()
                    fpc[u.slot] = dot_f32(fpc[u.slot], ainv_buf[...], precision=lax.Precision.HIGHEST)
                    if u.layer > 0:
                        ainv_copy(u.layer - 1).start()
                for g in range(3):
                    own_copy(u, g).start()
                    ag_copy(u, g, 3).start()
            return
        level = 8 - e
        for g in range(3):
            ag_copy(u, g, level).wait_recv()
            ag_copy(u, g, level).wait_send()
            if e == 5:
                own_copy(u, g).wait()
            if e < 8:
                ag_copy(u, g, level - 1).start()

    by_hook = {}
    for u in UNITS:
        for e, h in enumerate(u.hooks):
            by_hook.setdefault(h, []).append((u, e))

    def hook(index):
        for u, e in by_hook.get(index, []):
            event(u, e)

    def hooks_in_loop(phase, k):
        for i in range(NT):
            if by_hook.get(phase * NT + i):
                @pl.when(k == i)
                def _(i=i):
                    hook(phase * NT + i)

    def tile(k):
        return pl.ds(pl.multiple_of(k * tm, tm), tm)

    def x_copy(k):
        return pltpu.make_async_copy(x_hbm.at[tile(k), :], cur.at[tile(k), :], x_sem.at[k])

    def dy_copy(k, slot):
        return pltpu.make_async_copy(dy_hbm.at[tile(k), :], st_a.at[slot], sta_sem.at[slot])

    def hp_copy(layer, k, slot):
        src = x_hbm.at[tile(k), :] if layer == 0 else h_hbm.at[layer - 1, tile(k), :]
        return pltpu.make_async_copy(src, st_a.at[slot], sta_sem.at[slot])

    def zin_copy(layer, k, slot):
        return pltpu.make_async_copy(z_hbm.at[layer, tile(k), :], st_b.at[slot], stb_sem.at[slot])

    def zout_copy(layer, k, slot):
        return pltpu.make_async_copy(z_out.at[slot], z_hbm.at[layer, tile(k), :], z_sem.at[slot])

    def hout_copy(layer, k):
        return pltpu.make_async_copy(cur.at[tile(k), :], h_hbm.at[layer, tile(k), :], h_sem.at[k])

    def w_copy(layer, slot):
        return pltpu.make_async_copy(w_hbm.at[layer], w_buf.at[slot], w_sem.at[slot])

    def sym_add(slot, rows_t, rows_n):
        for j in range(4):
            part = dot_f32(rows_t[:B * (j + 1)], rows_n[:, B * j:B * (j + 1)]).reshape(j + 1, B, B)
            b0 = j * (j + 1) // 2
            sacc[slot, b0:b0 + j + 1] = sacc[slot, b0:b0 + j + 1] + part

    def full_add(slot, rows_t, read_cols):
        for j in range(4):
            cols = pl.ds(B * j, B)
            facc[slot, :, cols] = facc[slot, :, cols] + dot_f32(rows_t, read_cols(j))

    def loop(body):
        lax.fori_loop(0, NT, lambda k, c: (body(k), c)[1], 0)

    def clear_sym(slot):
        def body(i, carry):
            sacc[slot, i] = jnp.zeros((B, B), F32)
            return carry

        lax.fori_loop(0, NB + 1, body, 0)

    def clear_full(slot):
        def body(i, carry):
            facc[slot, pl.ds(pl.multiple_of(i * 64, 64), 64), :] = jnp.zeros((64, D), F32)
            return carry

        lax.fori_loop(0, D // 64, body, 0)

    for k in range(NT):
        x_copy(k).start()
    dy_copy(0, 0).start()
    w_copy(0, 0).start()
    w_copy(1, 1).start()

    barrier = pltpu.get_barrier_semaphore()
    for p in [core_peer] + peers:
        pl.semaphore_signal(barrier, inc=1, device_id=(p,), device_id_type=pl.DeviceIdType.MESH)
    pl.semaphore_wait(barrier, 4)

    clear_sym(0)
    clear_sym(1)

    def gram_dy(k):
        slot = lax.rem(k, 2)

        @pl.when(k + 1 < NT)
        def _():
            dy_copy(k + 1, 1 - slot).start()
        dy_copy(k, slot).wait()
        g = st_a[slot]
        sym_add(0, g.T, g)

    loop(gram_dy)

    def gram_x(k):
        hooks_in_loop(1, k)
        x_copy(k).wait()
        h = cur[tile(k), :]
        sym_add(1, h.T, h)

    loop(gram_x)

    for layer in range(3):
        phase = layer + 2
        wslot = layer % 2
        aslot = [2, 0, 1][layer]
        if layer > 0:
            w_copy(layer + 1, 1 - wslot).start()
        clear_sym(aslot)
        w_copy(layer, wslot).wait()

        def forward(k, layer=layer, phase=phase, wslot=wslot, aslot=aslot):
            hooks_in_loop(phase, k)
            slot = lax.rem(k, 2)

            @pl.when(k >= 2)
            def _():
                zout_copy(layer, k, slot).wait()
            h = cur[tile(k), :]
            for n in range(4):
                cols = pl.ds(B * n, B)
                z = dot_f32(h, w_buf[wslot, :, cols]).astype(BF16)
                z_out[slot, :, cols] = z
                zf = z.astype(F32)
                ht[:, cols] = (0.5 * zf * (1.0 + lax.erf(zf * ERF_SCALE))).astype(BF16)
            zout_copy(layer, k, slot).start()
            h2 = ht[...]
            sym_add(aslot, h2.T, h2)
            if layer > 0:
                hout_copy(layer - 1, k).wait()
            cur[tile(k), :] = ht[...]
            if layer < 2:
                hout_copy(layer, k).start()
            else:
                @pl.when(k == NT - 1)
                def _():
                    dy_copy(0, 0).start()

        loop(forward)
        zout_copy(layer, 0, 0).wait()
        zout_copy(layer, 1, 1).wait()

    clear_full(0)

    def top(k):
        hooks_in_loop(5, k)
        slot = lax.rem(k, 2)

        @pl.when(k + 1 < NT)
        def _():
            dy_copy(k + 1, 1 - slot).start()

        dy_copy(k, slot).wait()

        @pl.when(k == NT - 1)
        def _():
            hp_copy(2, 0, 0).start()
            zin_copy(2, 0, 0).start()

        g = st_a[slot]
        full_add(0, g.T, lambda j: cur[tile(k), pl.ds(B * j, B)])
        cur[tile(k), :] = st_a[slot]

    loop(top)

    for layer in (2, 1, 0):
        phase = 8 - layer
        wslot = [1, 0, 1][layer]
        sslot = [1, 0, 2][layer]
        fslot = [1, 0, 1][layer]
        if layer == 2:
            ainv_copy(3).start()
        if layer == 1:
            w_copy(1, 1).start()
        clear_sym(sslot)
        clear_full(fslot)
        if layer != 1:
            w_copy(layer + 1, wslot).wait()

        def backward(k, layer=layer, phase=phase, wslot=wslot, sslot=sslot, fslot=fslot):
            hooks_in_loop(phase, k)
            slot = lax.rem(k, 2)

            @pl.when(k + 1 < NT)
            def _():
                hp_copy(layer, k + 1, 1 - slot).start()
                zin_copy(layer, k + 1, 1 - slot).start()

            hp_copy(layer, k, slot).wait()
            zin_copy(layer, k, slot).wait()
            if layer > 0:
                @pl.when(k == NT - 1)
                def _():
                    hp_copy(layer - 1, 0, 0).start()
                    zin_copy(layer - 1, 0, 0).start()

            g_up = cur[tile(k), :]
            for n in range(4):
                cols = pl.ds(B * n, B)
                dh = dot_f32(g_up, w_buf[wslot, cols, :], ((1,), (1,))).astype(BF16)
                zf = st_b[slot, :, cols].astype(F32)
                slope = 0.5 * (1.0 + lax.erf(zf * ERF_SCALE)) + zf * jnp.exp(-0.5 * zf * zf) * PDF_SCALE
                ht[:, cols] = (dh.astype(F32) * slope).astype(BF16)
            g = ht[...]
            g_t = g.T
            sym_add(sslot, g_t, g)
            full_add(fslot, g_t, lambda j: st_a[slot, :, pl.ds(B * j, B)])
            cur[tile(k), :] = ht[...]

        loop(backward)

    first_last = 9 * NT
    n_last = max(max(max(u.hooks) for u in UNITS) + 1 - first_last, U_START + U_PIECES)

    def sinv_copy(layer):
        return pltpu.make_async_copy(sinv_hbm.at[layer], sinv_buf, sinv_sem)

    def vt_copy(layer, m, slot):
        return pltpu.make_async_copy(ovt.at[layer, :, pl.ds(pl.multiple_of(m * B, B), B)], vt_buf.at[slot], vt_sem.at[slot])

    def piece_of(p):
        return 3 - p // 2, 2 * lax.rem(p, 2) + core, lax.rem(p, 2)

    def u_at(layer, m):
        return u_hbm.at[layer, pl.ds(pl.multiple_of(m * B, B), B), :]

    def u_copy(layer, m):
        return pltpu.make_async_copy(u_buf, u_at(layer, m), u_sem)

    def u_send(layer, m, p):
        return pltpu.make_async_remote_copy(
            src_ref=u_buf, dst_ref=u_at(layer, m), send_sem=u_send_sem, recv_sem=u_recv_sem.at[p],
            device_id=(core_peer,), device_id_type=pl.DeviceIdType.MESH)

    sinv_copy(3).start()

    def final(s, carry):
        for i in range(n_last):
            if by_hook.get(first_last + i):
                @pl.when(s == i)
                def _(i=i):
                    hook(first_last + i)

        @pl.when((s + 1 >= U_START) & (s + 1 < U_START + U_PIECES))
        def _():
            vt_copy(*piece_of(s + 1 - U_START)).start()

        @pl.when((s >= U_START) & (s < U_START + U_PIECES))
        def _():
            p = s - U_START
            layer, m, slot = piece_of(p)

            @pl.when(slot == 0)
            def _():
                sinv_copy(layer).wait()

            vt_copy(layer, m, slot).wait()

            @pl.when(p > 0)
            def _():
                u_copy(layer, m).wait()
                u_send(layer, m, p).wait_send()
            for j in range(2):
                part = dot_f32(sinv_buf[512 * j:512 * (j + 1), :], vt_buf[slot], precision=lax.Precision.HIGHEST)
                u_buf[:, 512 * j:512 * (j + 1)] = part.T
            u_copy(layer, m).start()
            u_send(layer, m, p).start()

            @pl.when((slot == 1) & (layer > 0))
            def _():
                sinv_copy(layer - 1).start()
        return carry

    lax.fori_loop(0, n_last, final, 0)
    u_copy(0, core).wait()
    u_send(0, core, 0).wait_send()
    for p in range(U_PIECES):
        layer, m, _ = piece_of(p)
        u_send(layer, m, p).wait_recv()


def tail_kernel(sym_ref, u_ref, u_out, a_out, s_out):
    u_out[...] = u_ref[...]

    step = pl.program_id(0)

    def put(out_ref, half, row, col, blk):
        if row // (D // 2) == half:
            row = row - half * (D // 2)
            out_ref[0, row:row + blk.shape[0], col:col + blk.shape[1]] = blk

    def expand(out_ref, half):
        for b, (bi, bj) in enumerate(SYM_BLOCKS[:NB]):
            row, col = bi * B, bj * B
            if bi != bj:
                put(out_ref, half, row, col, sym_ref[0, b])
                put(out_ref, half, col, row, sym_ref[0, b].T)
            else:
                put(out_ref, half, row, col, sym_ref[0, b, :Q, :])
                put(out_ref, half, row + Q, col + Q, sym_ref[0, b, Q:, Q:])
                put(out_ref, half, row + Q, col, sym_ref[0, b, :Q, Q:].T)
                carried = sym_ref[0, b, Q:, :Q]
                c_row, c_col = CARRIED[bi]
                put(out_ref, half, 3 * B + c_row * Q, 3 * B + c_col * Q, carried)
                if c_row != c_col:
                    put(out_ref, half, 3 * B + c_col * Q, 3 * B + c_row * Q, carried.T)

    for half in range(2):
        @pl.when((step < 8) & (lax.rem(step, 2) == half))
        def _(half=half):
            expand(a_out, half)

        @pl.when((step >= 8) & (lax.rem(step, 2) == half))
        def _(half=half):
            expand(s_out, half)


def tail(osym, u_part):
    full = jax.ShapeDtypeStruct((4, D, D), F32)
    return pl.pallas_call(
        tail_kernel,
        grid=(16,),
        in_specs=[pl.BlockSpec((1, NB, B, B), lambda i: (i // 2, 0, 0, 0)), pl.BlockSpec((1, B, D), lambda i: (i // 4, i % 4, 0))],
        out_specs=(
            pl.BlockSpec((1, B, D), lambda i: (i // 4, i % 4, 0)),
            pl.BlockSpec((1, D // 2, D), lambda i: (jnp.minimum(i, 7) // 2, jnp.minimum(i, 7) % 2, 0)),
            pl.BlockSpec((1, D // 2, D), lambda i: (jnp.maximum(i - 8, 0) // 2, jnp.maximum(i - 8, 0) % 2, 0)),
        ),
        out_shape=(full, full, full),
        compiler_params=pltpu.CompilerParams(vmem_limit_bytes=48 * 1024 * 1024),
        name="tail_kernel",
    )(osym, u_part)


def solution(mesh):
    group_size = mesh.shape["data"]

    def local_step(x_loc, dy_loc, w_stack, a_old, s_old, a_inv, s_inv):
        n_rows = x_loc.shape[0]
        tm = n_rows // NT
        tokens = n_rows * group_size
        any_spec = pl.BlockSpec(memory_space=pl.ANY)
        vm = pltpu.VMEM
        osym, _, u_part, _, _ = pl.pallas_call(
            functools.partial(step_kernel, tm, float(tokens)),
            out_shape=(
                jax.ShapeDtypeStruct((8, NB, B, B), F32),
                jax.ShapeDtypeStruct((4, D, D), F32),
                jax.ShapeDtypeStruct((4, D, D), F32),
                jax.ShapeDtypeStruct((3, n_rows, D), BF16),
                jax.ShapeDtypeStruct((2, n_rows, D), BF16),
            ),
            in_specs=[any_spec] * 7,
            out_specs=(any_spec,) * 5,
            scratch_shapes=[
                vm((n_rows, D), BF16), vm((tm, D), BF16), vm((2, D, D), BF16), vm((2, tm, D), BF16), vm((2, tm, D), BF16),
                vm((D, D), F32), vm((D, D), F32), vm((2, D, B), F32), vm((B, D), F32),
                vm((3, NB + 1, B, B), F32), vm((2, D, D), F32),
                *[vm((3, NB, B >> i, B), F32) for i in range(1, 5)],
                *[vm((2, D >> i, D), F32) for i in range(1, 5)],
                vm((3, NB, 16, B), F32), vm((3, NB, 16, B), F32), vm((2, 64, D), F32),
                pltpu.SemaphoreType.DMA((5, 3)), pltpu.SemaphoreType.DMA((5, 8, 3)), pltpu.SemaphoreType.DMA((5, 3)),
                pltpu.SemaphoreType.DMA((3,)), pltpu.SemaphoreType.DMA((NT,)), pltpu.SemaphoreType.DMA((NT,)),
                pltpu.SemaphoreType.DMA((2,)), pltpu.SemaphoreType.DMA((2,)), pltpu.SemaphoreType.DMA((2,)),
                pltpu.SemaphoreType.DMA((2,)), pltpu.SemaphoreType.DMA, pltpu.SemaphoreType.DMA, pltpu.SemaphoreType.DMA((2,)), pltpu.SemaphoreType.DMA,
                pltpu.SemaphoreType.DMA, pltpu.SemaphoreType.DMA((U_PIECES,)),
            ],
            compiler_params=pltpu.CompilerParams(collective_id=0, has_side_effects=True, vmem_limit_bytes=67043328),
            name="step_kernel",
        )(x_loc, dy_loc, w_stack, a_old, s_old, a_inv, s_inv)
        return tail(osym, u_part)

    row_spec = P("data", None)
    full_spec = P()
    return jax.shard_map(local_step, mesh=mesh, in_specs=(row_spec, row_spec, full_spec, full_spec, full_spec, full_spec, full_spec), out_specs=(full_spec, full_spec, full_spec), check_vma=False)
```

profile of v0, /device:TPU:0, one launch (start us, length us, event | category | flops | bytes accessed | tf_op | source)
XLA Modules:
  0.0 339.3 jit_solution(14891225795955434867)
XLA Ops:
  0.6 302.4 %step_kernel.1 = (f32[8,9,256,256]{3,2,1,0:T(8,128)}, f32[4,1024,1024]{2,1,0:T(8,128)}, f32[4,1024,1024]{2,1,0:T(8,128)}, bf16[3,4096,1024]{2,1,0:T(8,128)(2,1)}, bf16[2,4096,1024]{2,1,0:T(8,128)(2,1)}) custom-call(bf16[4096,1024]{1,0:T(8,128)(2,1)} %x_hbm.1, bf16[4096,1024]{1,0:T(8,128)(2,1)} %dy_hbm.1, bf16[4,1024,1024]{2,1,0:T(8,128)(2,1)} %w_hbm.1, ...), custom_call_target="tpu_custom_call" | custom-call | tf_op jit(solution)/shard_map/step_kernel/pallas_call | solution.py:572
  303.0 36.3 %tail_kernel.1 = (f32[4,1024,1024]{2,1,0:T(8,128)}, f32[4,1024,1024]{2,1,0:T(8,128)}, f32[4,1024,1024]{2,1,0:T(8,128)}) custom-call(f32[8,9,256,256]{3,2,1,0:T(8,128)} %get-tuple-element.5.sym_ref, f32[4,1024,1024]{2,1,0:T(8,128)} %get-tuple-element.6.u_ref), custom_call_target="tpu_custom_call" | custom-call | tf_op jit(solution)/shard_map/tail_kernel/pallas_call | solution.py:548
where the time goes:
time: 340 us; the launch traced here: 339 us
  Pallas kernels  339 us (100%)
    pallas_call x1, Pallas kernels, local_step(): pl.pallas_call(functools.partial(step_kernel, tm, float(tokens)), out_sha...  302 us
    pallas_call x1, Pallas kernels, tail(): pl.pallas_call(tail_kernel, grid=(16,), in_specs=[pl.BlockSpec((1, NB, B,...  36.3 us

commit v1 on v0

--- a/solution.py
+++ b/solution.py
@@ -44,21 +44,21 @@
 
 
 U_PIECES = 8
-U_START = 22
+U_START = 13
 
 UNITS = [
-    Unit("s", 3, 0, 9, "35421232", 0),
-    Unit("a", 1, 2, 26, "74222784", 0),
-    Unit("a", 3, 1, 42, "46315283", 0),
-    Unit("w", 3, 0, 48, "03311151", 0),
-    Unit("s", 1, 0, 67, "08993561", 0),
-    Unit("a", 0, 1, 16, "14222462", 0),
-    Unit("a", 2, 0, 34, "13223984", 0),
-    Unit("s", 0, 1, 79, "53542257", 0),
-    Unit("w", 0, 1, 76, "16174220", 0),
-    Unit("w", 1, 0, 64, "12782571", 2),
-    Unit("w", 2, 1, 56, "03311143", 1),
-    Unit("s", 2, 2, 68, "08579225", 0),
+    Unit("s", 0, 1, 77, "22214224", 0),
+    Unit("w", 1, 0, 67, "28321131", 2),
+    Unit("a", 3, 1, 42, "76223118", 0),
+    Unit("w", 2, 1, 56, "23111246", 1),
+    Unit("a", 1, 2, 28, "24522365", 0),
+    Unit("w", 3, 0, 48, "23111244", 0),
+    Unit("s", 1, 0, 65, "37713328", 0),
+    Unit("a", 2, 0, 34, "27542130", 0),
+    Unit("a", 0, 1, 17, "63223233", 0),
+    Unit("w", 0, 1, 77, "31111321", 0),
+    Unit("s", 2, 2, 61, "37734322", 0),
+    Unit("s", 3, 0, 8, "83213233", 0),
 ]
 
 

time: 340 us -> 329 us (0.968)
  Pallas kernels: 339 us -> 328 us
    pallas_call x1, Pallas kernels: 302 us -> 291 us  [local_step(): pl.pallas_call(functools.partial(step_kernel, tm, float(tokens)), out_sha...]
where the time goes in v1:
time: 329 us; the launch traced here: 328 us
  Pallas kernels  328 us (100%)
    pallas_call x1, Pallas kernels, local_step(): pl.pallas_call(functools.partial(step_kernel, tm, float(tokens)), out_sha...  291 us
    pallas_call x1, Pallas kernels, tail(): pl.pallas_call(tail_kernel, grid=(16,), in_specs=[pl.BlockSpec((1, NB, B,...  36.3 us

profile of v1, /device:TPU:0, one launch (start us, length us, event | category | flops | bytes accessed | tf_op | source)
XLA Modules:
  0.0 328.3 jit_solution(8615019763733747396)
XLA Ops:
  0.6 291.4 %step_kernel.1 = (f32[8,9,256,256]{3,2,1,0:T(8,128)}, f32[4,1024,1024]{2,1,0:T(8,128)}, f32[4,1024,1024]{2,1,0:T(8,128)}, bf16[3,4096,1024]{2,1,0:T(8,128)(2,1)}, bf16[2,4096,1024]{2,1,0:T(8,128)(2,1)}) custom-call(bf16[4096,1024]{1,0:T(8,128)(2,1)} %x_hbm.1, bf16[4096,1024]{1,0:T(8,128)(2,1)} %dy_hbm.1, bf16[4,1024,1024]{2,1,0:T(8,128)(2,1)} %w_hbm.1, ...), custom_call_target="tpu_custom_call" | custom-call | tf_op jit(solution)/shard_map/step_kernel/pallas_call | solution.py:572
  292.0 36.3 %tail_kernel.1 = (f32[4,1024,1024]{2,1,0:T(8,128)}, f32[4,1024,1024]{2,1,0:T(8,128)}, f32[4,1024,1024]{2,1,0:T(8,128)}) custom-call(f32[8,9,256,256]{3,2,1,0:T(8,128)} %get-tuple-element.5.sym_ref, f32[4,1024,1024]{2,1,0:T(8,128)} %get-tuple-element.6.u_ref), custom_call_target="tpu_custom_call" | custom-call | tf_op jit(solution)/shard_map/tail_kernel/pallas_call | solution.py:548
